TPU v7x, 128 devices: a whole 4x4x4 slice. The times are simulated.
128 devices in a mesh: enc: 8 (over z, core), ctx: 16 (over y, x).
Axes of the slice: x: 4, y: 4, z: 4, core: 2. Of those that a mesh axis runs over, the one named last changes fastest.
Arguments:
- patches: bfloat16 [6144, 1280], P('enc'), may hold values from -17 to 17
- patch_image: int32 [6144], P('enc'), may hold values from 63 to 1535, as said below
- vit_gain: float32 [1280], replicated, may hold values from 0.1 to 1.9
- vit_qkv: bfloat16 [1280, 16, 240], P(None, 'ctx')
- vit_proj: bfloat16 [1280, 1280], P('ctx'), may hold values from -0.15625 to 0.15625
- merge_gain: float32 [1280], replicated, may hold values from 0.1 to 1.9
- merge_up: bfloat16 [5120, 5120], P(None, 'ctx'), may hold values from -0.078125 to 0.078125
- merge_down: bfloat16 [5120, 8192], P('ctx', 'enc'), may hold values from -0.078125 to 0.078125
- text_embed: bfloat16 [6144, 8192], P('ctx', 'enc'), may hold values from -17 to 17
- placeholder_unit: int32 [6144], replicated, may hold values from -1 to 1535, as said below
- doc_id: int32 [6144], replicated, may hold values from 0 to 31, never falling along the last dimension, each value on 1 to 3456 neighbouring positions
- dec_gain: float32 [8192], replicated, may hold values from 0.1 to 1.9
- dec_wq: bfloat16 [8192, 4096], P(None, 'enc')
- dec_wk: bfloat16 [8192, 1024], P(None, 'enc')
- dec_wv: bfloat16 [8192, 1024], P(None, 'enc'), may hold values from -0.0625 to 0.0625
Outputs:
- attended: bfloat16 [6144, 4096], P('ctx', 'enc')
Inputs may be any that keep to these rules, and one draw needn't show every extreme that they name: `patch_image`: the patches of an image are consecutive, start at a multiple of 4, number a multiple of 4 and at most 256, and lie within one aligned block of 768 patches; image numbers never fall and differ between images; in every such block some image has exactly 256 patches. `placeholder_unit`: -1 marks a text position. Every unit appears exactly once; the units of one image fill consecutive placeholders in their order; the placeholders of an aligned block of 384 positions are consecutive and number at most 192, and some block holds exactly 192. `doc_id`: document numbers never fall; a document has at most 3456 positions, and some document exactly 3456.
All inputs are finite; a program needn't handle non-finite values.
Results may differ from a plain program's by a relative error of at most 0.0085.
Values may be sent and summed in bfloat16 or wider, within the bound.
A program may use at most 128 MiB of HBM per device.

v0:
```python
import math
import jax
import jax.numpy as jnp
from jax import lax
from jax.sharding import PartitionSpec as P

HD = 128
QPK = 4
EPSILON = 1e-06
NEGATIVE = -1e30


def in_blocks(x, dim, size):
    dims = x.shape
    blocks = x.reshape(*dims[:dim], size, dims[dim] // size, *dims[dim + 1 :])
    return jnp.moveaxis(blocks, dim, 0)


def sent_and_summed(x, axis, dim):
    blocks = in_blocks(x, dim, lax.axis_size(axis))
    arrived = lax.all_to_all(blocks, axis, split_axis=0, concat_axis=0, tiled=True)
    return arrived.sum(axis=0)


def in_order(blocks, dim):
    dims = list(blocks.shape[1:])
    dims[dim] *= blocks.shape[0]
    return jnp.moveaxis(blocks, 0, dim).reshape(dims)


def sent_to_all(x, axis):
    size = lax.axis_size(axis)
    return lax.all_to_all(jnp.broadcast_to(x[None], (size, *x.shape)), axis, 0, 0, tiled=True)


def gathered_copies(x, axis, dim):
    return in_order(sent_to_all(x, axis), dim)


def of_everyone(x, axis):
    return sent_to_all(x, axis).sum(axis=0)


def in_one_piece(arrays, axis, dim, along):
    widths = [a.shape[along] for a in arrays]
    both = jnp.concatenate(arrays, axis=along)
    result = lax.all_gather(both, axis, axis=dim, tiled=True)
    return tuple(jnp.split(result, [sum(widths[:k]) for k in range(1, len(widths))], axis=along))


def layer_norm(values, scaling):
    widened = values.astype(jnp.float32)
    center = widened - jnp.mean(widened, axis=1, keepdims=True)
    spread = jnp.mean(center * center, axis=1, keepdims=True)
    return (center * lax.rsqrt(spread + EPSILON) * scaling).astype(jnp.bfloat16)


def image_attention(queries, keys_in, values_in, image_ids):
    head_count, row_count, head_width = queries.shape
    block_rows = math.gcd(row_count, 512)
    scaling = head_width ** (-0.5)

    def image_one_block(offset):
        query_block = lax.dynamic_slice_in_dim(queries, offset, block_rows, 1)
        block_ids = lax.dynamic_slice_in_dim(image_ids, offset, block_rows, 0)
        allowed = block_ids[:, None] == image_ids[None, :]
        scores = (
            jnp.einsum("hqd,hkd->hqk", query_block, keys_in, preferred_element_type=jnp.float32)
            * scaling
        )
        scores = jnp.where(allowed[None], scores, NEGATIVE)
        highest = jnp.max(scores, axis=2, keepdims=True)
        weights = jnp.exp(scores - highest)
        totals = jnp.sum(weights, axis=2, keepdims=True)
        mixture = jnp.einsum(
            "hqk,hkd->hqd",
            weights.astype(jnp.bfloat16),
            values_in,
            preferred_element_type=jnp.float32,
        )
        return (mixture / totals).astype(jnp.bfloat16)

    offsets = jnp.arange(row_count // block_rows, dtype=jnp.int32) * block_rows
    blocks = lax.map(image_one_block, offsets)
    return blocks.transpose(1, 0, 2, 3).reshape(head_count, row_count, head_width)


def body(
    patches,
    patch_image,
    vit_gain,
    vit_qkv,
    vit_proj,
    merge_gain,
    merge_up,
    merge_down,
    text_embed,
    placeholder_unit,
    doc_id,
    dec_gain,
    dec_wq,
    dec_wk,
    dec_wv,
):
    ctx_count = lax.axis_size("ctx")
    enc_count = lax.axis_size("enc")
    ctx_index = lax.axis_index("ctx")
    group_rows = patches.shape[0]
    head_count = vit_qkv.shape[1]
    head_width = vit_qkv.shape[2] // 3
    normed_patches = layer_norm(patches, vit_gain)
    packed = jnp.dot(
        normed_patches,
        vit_qkv.reshape(vit_qkv.shape[0], head_count * 3 * head_width),
        preferred_element_type=jnp.float32,
    )
    packed = (
        packed.astype(jnp.bfloat16)
        .reshape(group_rows, head_count, 3, head_width)
        .transpose(2, 1, 0, 3)
    )
    attended_patches = image_attention(packed[0], packed[1], packed[2], patch_image)
    flat_heads = attended_patches.transpose(1, 0, 2).reshape(group_rows, head_count * head_width)
    head_terms = jnp.dot(flat_heads, vit_proj, preferred_element_type=jnp.float32)
    share_sum = sent_and_summed(head_terms, "ctx", 0)
    share_count = share_sum.shape[0]
    own_rows = lax.dynamic_slice_in_dim(patches, ctx_index * share_count, share_count, 0)
    own_out = (own_rows.astype(jnp.float32) + share_sum).astype(jnp.bfloat16)
    own_normed = layer_norm(lax.optimization_barrier(own_out), merge_gain)
    merge_input = gathered_copies(own_normed, "ctx", 0)
    unit_inputs = merge_input.reshape(group_rows // 4, 4 * merge_input.shape[1])
    hidden = jax.nn.gelu(
        jnp.dot(unit_inputs, merge_up, preferred_element_type=jnp.float32), approximate=False
    ).astype(jnp.bfloat16)
    all_hidden = gathered_copies(hidden, "enc", 0)
    unit_total = all_hidden.shape[0]
    tok_rows = text_embed.shape[0]
    feature_cols = text_embed.shape[1]
    local_units = lax.dynamic_slice_in_dim(placeholder_unit, ctx_index * tok_rows, tok_rows, 0)
    present = local_units >= 0
    slot_rows = tok_rows // 2
    shard_units = placeholder_unit.reshape(ctx_count, tok_rows)
    shard_present = shard_units >= 0
    shard_rank = jnp.cumsum(shard_present.astype(jnp.int32), axis=1) - 1
    matches = shard_present[:, None, :] & (
        shard_rank[:, None, :] == jnp.arange(slot_rows, dtype=jnp.int32)[None, :, None]
    )
    slot_units = (jnp.sum(jnp.where(matches, shard_units[:, None, :] + 1, 0), axis=2) - 1).reshape(
        -1
    )
    picked = jnp.take(all_hidden, jnp.clip(slot_units, 0, unit_total - 1), axis=0)
    picked = jnp.where((slot_units >= 0)[:, None], picked, jnp.zeros_like(picked))
    arrived = lax.psum_scatter(
        jnp.dot(picked, merge_down, preferred_element_type=jnp.float32),
        "ctx",
        scatter_dimension=0,
        tiled=True,
    ).astype(jnp.bfloat16)
    local_rank = jnp.cumsum(present.astype(jnp.int32)) - 1
    vision_local = jnp.take(arrived, jnp.clip(local_rank, 0, slot_rows - 1), axis=0)
    sequence = jnp.where(present[:, None], vision_local, text_embed)
    local_wide = sequence.astype(jnp.float32)
    squares = of_everyone(jnp.sum(local_wide * local_wide, axis=1), "enc")
    row_scale = lax.rsqrt(squares / (feature_cols * enc_count) + EPSILON)
    start_state = (
        jnp.zeros((tok_rows, dec_wq.shape[1]), jnp.float32),
        jnp.zeros((tok_rows, dec_wk.shape[1]), jnp.float32),
        jnp.zeros((tok_rows, dec_wv.shape[1]), jnp.float32),
    )
    normed_part = (
        lax.all_gather(sequence, "enc", axis=1, tiled=True).astype(jnp.float32)
        * row_scale[:, None]
        * dec_gain
    ).astype(jnp.bfloat16)
    query_part = jnp.dot(normed_part, dec_wq, preferred_element_type=jnp.float32)
    key_part = jnp.dot(normed_part, dec_wk, preferred_element_type=jnp.float32)
    value_part = jnp.dot(normed_part, dec_wv, preferred_element_type=jnp.float32)
    queries_flat = query_part.astype(jnp.bfloat16)
    keys_local = key_part.astype(jnp.bfloat16)
    values_local = value_part.astype(jnp.bfloat16)
    kv_local = dec_wk.shape[1] // HD
    queries = queries_flat.reshape(tok_rows, kv_local, QPK, HD).transpose(1, 2, 0, 3)
    query_first = ctx_index * tok_rows
    query_pos = query_first + jnp.arange(tok_rows, dtype=jnp.int32)
    query_docs = lax.dynamic_slice_in_dim(doc_id, query_first, tok_rows, 0)
    scaling = HD ** (-0.5)
    start_state = (
        jnp.full((kv_local, QPK, tok_rows), NEGATIVE, jnp.float32),
        jnp.zeros((kv_local, QPK, tok_rows), jnp.float32),
        jnp.zeros((kv_local, QPK, tok_rows, HD), jnp.float32),
    )
    offset = jnp.int32(0)
    key_part, value_part = in_one_piece((keys_local, values_local), "ctx", 0, 1)
    key_count = key_part.shape[0]
    sub_rows = math.gcd(key_count, 512)
    last_doc = lax.dynamic_slice_in_dim(doc_id, offset + key_count - 1, 1, 0)[0]
    visible = (offset <= query_first + tok_rows - 1) & (last_doc >= query_docs[0])

    def update(current):

        def update_one_block(turn_index, inner_state):
            highest, totals, mixture = inner_state
            begin_row = turn_index * sub_rows
            keys_block = lax.dynamic_slice_in_dim(key_part, begin_row, sub_rows, 0).reshape(
                sub_rows, kv_local, HD
            )
            values_block = lax.dynamic_slice_in_dim(value_part, begin_row, sub_rows, 0).reshape(
                sub_rows, kv_local, HD
            )
            key_pos = begin_row + jnp.arange(sub_rows, dtype=jnp.int32)
            key_docs = lax.dynamic_slice_in_dim(doc_id, begin_row, sub_rows, 0)
            allowed = (key_pos[None, :] <= query_pos[:, None]) & (
                key_docs[None, :] == query_docs[:, None]
            )
            scores = (
                jnp.einsum(
                    "gjtd,sgd->gjts", queries, keys_block, preferred_element_type=jnp.float32
                )
                * scaling
            )
            new_peak = jnp.maximum(highest, jnp.max(jnp.where(allowed, scores, NEGATIVE), axis=3))
            factor = jnp.exp(highest - new_peak)
            weights = jnp.where(allowed, jnp.exp(scores - new_peak[..., None]), 0.0)
            totals = totals * factor + jnp.sum(weights, axis=3)
            mixture = mixture * factor[..., None] + jnp.einsum(
                "gjts,sgd->gjtd",
                weights.astype(jnp.bfloat16),
                values_block,
                preferred_element_type=jnp.float32,
            )
            return (new_peak, totals, mixture)

        return lax.fori_loop(0, key_count // sub_rows, update_one_block, current)

    def unchanged(current):
        return current

    finished = lax.cond(visible, update, unchanged, start_state)
    outputs = (finished[2] / finished[1][..., None]).astype(jnp.bfloat16)
    return outputs.transpose(2, 0, 1, 3).reshape(tok_rows, kv_local * QPK * HD)


def solution(mesh):
    placed = (
        P("enc", None),
        P("enc"),
        P(),
        P(None, "ctx", None),
        P("ctx", None),
        P(),
        P(None, "ctx"),
        P("ctx", "enc"),
        P("ctx", "enc"),
        P(),
        P(),
        P(),
        P(None, "enc"),
        P(None, "enc"),
        P(None, "enc"),
    )
    return jax.shard_map(
        body, mesh=mesh, in_specs=placed, out_specs=P("ctx", "enc"), check_vma=False
    )
```

profile of v0, /device:TPU:0, one launch (start us, length us, event | category | flops | bytes accessed | tf_op | source)
XLA Modules:
  0.0 493.8 jit_solution(5505292122462072174)
XLA Ops:
  6.6 2.0 convert_reduce_fusion
  11.3 2.0 copy.40
  13.3 1.9 slice_bitcast_fusion
  15.2 16.2 %while.28 = (s32[]{:T(128)}, bf16[3,1,256,80]{2,3,1,0:T(8,128)(2,1)}, s32[3]{0:T(128)S(1)}, s32[768]{0:T(1024)S(1)}, bf16[1,768,80]{2,1,0:T(8,128)(2,1)}, /*inde...) while((s32[]{:T(128)}, ...), condition=%wide.region_10.11_spmd, body=%wide.region_7.10_spmd.sunk | while | flops 64527876 | bytes 2797211 | solution.py:84
  32.5 3.5 fusion.79
  36.0 7.2 %all-to-all-start = ((f32[16,48,1280]{2,1,0:T(8,128)}), f32[16,48,1280]{2,1,0:T(8,128)}, u32[]{:S(2)}, u32[]{:S(2)}) async-start(f32[16,48,1280]{2,1,0:T(8,128)} %fusion.79), calls=%async_computation | async-start | bytes 7864320 | tf_op jit(solution)/shard_map/all_to_all | solution.py:21
  43.2 59.5 %all-to-all-done = f32[16,48,1280]{2,1,0:T(8,128)} async-done(((f32[16,48,1280]{2,1,0:T(8,128)}), f32[16,48,1280]{2,1,0:T(8,128)}, u32[]{:S(2)}, u32[]{:S(2)}) %all-to-all-start) | async-done | bytes 3932192 | tf_op jit(solution)/shard_map/all_to_all | solution.py:21
  102.7 2.3 reduce_sum.97
  107.9 4.5 all-to-all-start.1
  115.6 24.9 %all-to-all-done.1 = bf16[16,48,1280]{2,1,0:T(8,128)(2,1)} async-done(((bf16[16,48,1280]{2,1,0:T(8,128)(2,1)}), bf16[16,48,1280]{2,1,0:T(8,128)(2,1)}, u32[]{:S(2)}, u32[]{:S(2)}) %all-to-all-start.1) | async-done | bytes 1966112 | tf_op jit(solution)/shard_map/all_to_all | solution.py:33
  140.5 4.1 reshape_reshape.3
  144.6 3.6 fusion.66
  149.3 5.3 %all-to-all-start.2 = ((bf16[8,192,320]{2,1,0:T(8,128)(2,1)}), bf16[8,192,320]{2,1,0:T(8,128)(2,1)S(1)}, u32[]{:S(2)}, u32[]{:S(2)}) async-start(bf16[8,192,320]{2,1,0:T(8,128)(2,1)} %broadcast_in_dim.158), calls=%async_computation.2 | async-start | bytes 2359296 | tf_op jit(solution)/shard_map/all_to_all | solution.py:33
  154.7 17.3 %all-to-all-done.2 = bf16[8,192,320]{2,1,0:T(8,128)(2,1)S(1)} async-done(((bf16[8,192,320]{2,1,0:T(8,128)(2,1)}), bf16[8,192,320]{2,1,0:T(8,128)(2,1)S(1)}, u32[]{:S(2)}, u32[]{:S(2)}) %all-to-all-start.2) | async-done | bytes 983072 | tf_op jit(solution)/shard_map/all_to_all | solution.py:33
  171.9 11.0 %gather_fusion = bf16[3072,320]{1,0:T(8,128)(2,1)S(1)} fusion(bf16[1536,320]{1,0:T(8,128)(2,1)S(1)} %bitcast.146, s32[3072]{0:T(1024)S(1)} %broadcast_clamp_fusion), kind=kCustom, calls=%fused_computation | custom fusion | bytes 3944448 | tf_op jit(solution)/shard_map/jit(_take)/gather | solution.py:151
  182.9 7.6 %fusion.47 = f32[3072,1024]{1,0:T(8,128)} fusion(bf16[320,1024]{1,0:T(8,128)(2,1)} %param.28, bf16[3072,320]{1,0:T(8,128)(2,1)S(1)} %gather_fusion, pred[3072]{0:T(1024)(128)(4,1)} %compare_and_fusion.1, pred[3072]{0:T(1024)(128)(4,1)S(1)} %ge.77), kind=kOutput, calls=%fused_computation.61 | convolution fusion | flops 2015232000 | bytes 15210496 | tf_op jit(solution)/shard_map/dot_general | solution.py:154
  192.2 88.8 %reduce-scatter.2.cloned.1.call-done = f32[192,1024]{1,0:T(8,128)} async-done(((f32[3072,1024]{1,0:T(8,128)}), f32[192,1024]{1,0:T(8,128)}) %reduce-scatter.2.cloned.1.call-update) | async-done | bytes 786448 | tf_op jit(solution)/shard_map/reduce_scatter | solution.py:153
  282.2 2.1 gather_fusion.1
  285.7 9.6 %all_to_all.21 = f32[8,1,384]{2,1,0:T(1,128)S(1)} all-to-all(f32[8,1,384]{2,1,0:T(1,128)S(1)} %broadcast_in_dim.162), channel_id=1, replica_groups=mesh['enc'=8,'ctx'=16] {'enc'}, dimensions={0} | all-to-all | bytes 24576 | tf_op jit(solution)/shard_map/all_to_all | solution.py:33
  295.3 30.6 %all-gather.3.cloned.1.call-done = bf16[384,8192]{1,0:T(8,128)(2,1)} async-done(((bf16[384,1024]{1,0:T(8,128)(2,1)}), bf16[384,8192]{1,0:T(8,128)(2,1)}) %all-gather.3.cloned.1.call-update) | async-done | bytes 6291472 | tf_op jit(solution)/shard_map/all_gather | solution.py:171
  325.9 5.7 %convolution_convert_fusion.2 = bf16[384,128]{0,1:T(8,128)(2,1)S(1)} fusion(bf16[8192,128]{1,0:T(8,128)(2,1)} %param.34, bf16[384,8192]{1,0:T(8,128)(2,1)} %all-gather.3.cloned.1.call-done, f32[8192]{0:T(1024)S(1)} %copy-done.10, f32[384]{0:T(512)S(1)} %add_rsqrt_fusion.1), kind=kOutput, calls=%fused_computation.76 | convolution fusion | flops 817938432 | bytes 8521216 | tf_op jit(solution)/shard_map/dot_general | solution.py:176
  331.7 2.2 convolution_convert_fusion.1
  338.5 8.7 %convolution_convert_fusion = bf16[384,512]{1,0:T(8,128)(2,1)S(1)} fusion(bf16[8192,512]{1,0:T(8,128)(2,1)} %param.33, bf16[384,8192]{1,0:T(8,128)(2,1)} %all-gather.3.cloned.1.call-done, f32[8192]{0:T(1024)S(1)} %copy-done.10, f32[384]{0:T(512)S(1)} %add_rsqrt_fusion.1), kind=kOutput, calls=%fused_computation.71 | convolution fusion | flops 3234004992 | bytes 15107584 | tf_op jit(solution)/shard_map/dot_general | solution.py:175
  348.1 38.2 %all-gather.5.cloned.1.call-done = bf16[6144,256]{0,1:T(8,128)(2,1)} async-done(((bf16[384,256]{0,1:T(8,128)(2,1)}), bf16[6144,256]{0,1:T(8,128)(2,1)}) %all-gather.5.cloned.1.call-update) | async-done | bytes 3145744 | tf_op jit(solution)/shard_map/all_gather | solution.py:47
  386.4 98.2 %conditional.1 = (f32[1,4,384]{2,1,0:T(4,128)}, f32[1,4,384,128]{3,2,1,0:T(8,128)}) conditional(s32[]{:T(128)} %convert_element_type.75, () %tuple.31, (bf16[6144,256]{0,1:T(8,128)(2,1)}, s32[]{:T(128)}, s32[384]{0:T(512)S(1)}, s32[6144]{0:T(1024)}, s32[384]{0:T(512)S(1)}, /*index=5*/bf16[1,4,384,128]{3,2,1,0:T(8,128)(2,1)}) %tuple.87), branch_computations={%region_17.18_spmd, %region_18.23_spmd} | conditional | flops 412493696 | bytes 25149788 | solution.py:238
  386.4 3.2 copy.44
  389.5 1.9 fusion.87
  391.4 93.2 %while.27 = (s32[]{:T(128)}, f32[1,4,384]{2,1,0:T(4,128)S(1)}, f32[1,4,384]{2,1,0:T(4,128)}, f32[1,4,384,128]{3,2,1,0:T(8,128)}, s32[384]{0:T(512)S(1)}, /*index...) while((s32[]{:T(128)}, f32[1,4,384]{2,1,0:T(4,128)S(1)}, ...), condition=%wide.region_22.22_spmd.clone, body=%wide.region_19.21_spmd.clone.sunk | while | flops 412493312 | bytes 12563663 | solution.py:233
  394.2 2.8 fusion.116
  401.0 3.1 fusion.116
  408.9 3.1 fusion.116
  416.7 3.1 fusion.116
  422.8 1.7 fusion.113
  424.6 3.1 fusion.116
  430.6 1.7 fusion.113
  432.4 3.1 fusion.116
  438.5 1.7 fusion.113
  440.3 3.1 fusion.116
  446.3 1.7 fusion.113
  448.1 3.1 fusion.116
  454.2 1.7 fusion.113
  456.0 3.1 fusion.116
  462.0 1.7 fusion.113
  463.8 3.1 fusion.116
  469.9 1.7 fusion.113
  471.7 3.1 fusion.116
  477.7 1.7 fusion.113
  479.5 3.1 fusion.116
  (195 shorter events, 73.9 us)
Async XLA Ops:
  6.5 138.1 %copy-start = (bf16[5120,320]{0,1:T(8,128)(2,1)S(1)}, bf16[5120,320]{0,1:T(8,128)(2,1)}, u32[]{:S(2)}) copy-start(bf16[5120,320]{0,1:T(8,128)(2,1)} %param.27) | copy-start | bytes 9830404
  6.5 3.0 copy-start.11
  6.5 2.3 copy-start.2
  6.5 3.0 copy-start.9
  9.5 5.7 %copy-start.6 = (s32[768]{0:T(1024)S(1)}, s32[768]{0:T(1024)}, u32[]{:S(2)}) copy-start(s32[768]{0:T(1024)} %param.22) | copy-start | bytes 9220
  36.0 66.7 %all-to-all-start = ((f32[16,48,1280]{2,1,0:T(8,128)}), f32[16,48,1280]{2,1,0:T(8,128)}, u32[]{:S(2)}, u32[]{:S(2)}) async-start(f32[16,48,1280]{2,1,0:T(8,128)} %fusion.79), calls=%async_computation | async-start | bytes 7864320 | tf_op jit(solution)/shard_map/all_to_all | solution.py:21
  43.2 63.2 %copy-start.5 = (f32[1280]{0:T(1024)S(1)}, f32[1280]{0:T(1024)}, u32[]{:S(2)}) copy-start(f32[1280]{0:T(1024)} %param.26) | copy-start | bytes 15364
  106.3 6.0 %copy-start.4 = (s32[6144]{0:T(1024)S(1)}, s32[6144]{0:T(1024)}, u32[]{:S(2)}) copy-start(s32[6144]{0:T(1024)} %param.30) | copy-start | bytes 73732
  107.9 32.7 %all-to-all-start.1 = ((bf16[16,48,1280]{2,1,0:T(8,128)(2,1)}), bf16[16,48,1280]{2,1,0:T(8,128)(2,1)}, u32[]{:S(2)}, u32[]{:S(2)}) async-start(bf16[16,48,1280]{2,1,0:T(8,128)(2,1)} %broadcast_in_dim.157), calls=%async_computation.1 | async-start | bytes 3932160 | tf_op jit(solution)/shard_map/all_to_all | solution.py:33
  149.3 22.6 %all-to-all-start.2 = ((bf16[8,192,320]{2,1,0:T(8,128)(2,1)}), bf16[8,192,320]{2,1,0:T(8,128)(2,1)S(1)}, u32[]{:S(2)}, u32[]{:S(2)}) async-start(bf16[8,192,320]{2,1,0:T(8,128)(2,1)} %broadcast_in_dim.158), calls=%async_computation.2 | async-start | bytes 2359296 | tf_op jit(solution)/shard_map/all_to_all | solution.py:33
  154.6 126.4 %reduce-scatter.2.cloned.1.call-start = ((), (), s32[]{:S(2)}) async-start(), calls=%async_computation.5 | async-start | bytes 13369344 | tf_op jit(solution)/shard_map/reduce_scatter | solution.py:153
  190.6 135.3 %all-gather.3.cloned.1.call-start = ((), (), s32[]{:S(2)}) async-start(), calls=%async_computation.6 | async-start | bytes 7077888 | tf_op jit(solution)/shard_map/all_gather | solution.py:171
  282.1 2.1 copy-start.3
  284.2 41.7 %copy-start.10 = (f32[8192]{0:T(1024)S(1)}, f32[8192]{0:T(1024)}, u32[]{:S(2)}) copy-start(f32[8192]{0:T(1024)} %param.32) | copy-start | bytes 98308
  285.6 100.7 %all-gather.5.cloned.1.call-start = ((), (), s32[]{:S(2)}) async-start(), calls=%async_computation.7 | async-start | bytes 3342336 | tf_op jit(solution)/shard_map/all_gather | solution.py:47
  295.3 36.3 %copy-start.8 = (bf16[8192,128]{1,0:T(8,128)(2,1)S(1)}, bf16[8192,128]{1,0:T(8,128)(2,1)}, u32[]{:S(2)}) copy-start(bf16[8192,128]{1,0:T(8,128)(2,1)} %param.35) | copy-start | bytes 6291460
  325.9 5.7 %copy-start.7 = (bf16[384,8192]{1,0:T(8,128)(2,1)S(1)}, bf16[384,8192]{1,0:T(8,128)(2,1)}, u32[]{:S(2)}) copy-start(bf16[384,8192]{1,0:T(8,128)(2,1)} %all-gather.3.cloned.1.call-done) | copy-start | bytes 18874372
  484.6 2.7 copy-start.1
Sparse Core Ops, SparseCore 0:
  190.7 90.2 reduce-scatter.1
  285.8 40.1 all-gather.2
  334.7 51.5 all-gather.4
where the time goes:
time: 496 us; the launch traced here: 494 us
  waiting for transfers between devices  259 us (52%)
  matrix products  97.8 us (20%)
  local copies, waits for them, and re-layouts  46.6 us (9%)
  other arithmetic  41.9 us (8%)
  starting transfers between devices  17.1 us (3%)
  between operations  14.8 us (3%)
  blocking collectives  9.58 us (2%)
  loops' own time  6.57 us (1%)
    reduce_scatter x1, waiting for transfers between devices, body(): lax.psum_scatter(jnp.dot(picked, merge_down, preferred_element_type=jnp.f...  88.8 us
    all_to_all x1, waiting for transfers between devices, sent_and_summed(): lax.all_to_all(blocks, axis, split_axis=0, concat_axis=0, tiled=True)  59.5 us
    all_to_all x2, waiting for transfers between devices, sent_to_all(): lax.all_to_all(jnp.broadcast_to(x[None], (size, *x.shape)), axis, 0, 0, t...  42.2 us
    all_gather x1, waiting for transfers between devices, in_one_piece(): result = lax.all_gather(both, axis, axis=dim, tiled=True)  38.2 us
    dot_general x12, matrix products, update_one_block(): jnp.einsum('gjts,sgd->gjtd', weights.astype(jnp.bfloat16), values_block,...  36.9 us
    all_gather x1, waiting for transfers between devices, body(): lax.all_gather(sequence, 'enc', axis=1, tiled=True).astype(jnp.float32)  30.6 us
    dot_general x12, matrix products, update_one_block(): jnp.einsum('gjtd,sgd->gjts', queries, keys_block, preferred_element_type=...  20.9 us
    add x12, other arithmetic, update_one_block(): totals = totals * factor + jnp.sum(weights, axis=3)  14.8 us
  transfers between devices with their start and end apart: 6, of which 6 were waited for; matrix products, arithmetic and copies ran while one was open for 3% of the time, Pallas kernels for 0%

commit v1 on v0

--- a/solution.py
+++ b/solution.py
@@ -102,6 +102,14 @@
     dec_wk,
     dec_wv,
 ):
+
+    def press_columns_now(sample, which_axis):
+        formed = lax.axis_size(which_axis)
+        seen_now = jnp.stack(formed * [sample])
+        k_now = lax.all_to_all(seen_now, which_axis, 0, 0)
+        a_now = jnp.concatenate(k_now, 1)
+        return a_now
+
     ctx_count = lax.axis_size("ctx")
     enc_count = lax.axis_size("enc")
     ctx_index = lax.axis_index("ctx")
@@ -168,7 +176,7 @@
         jnp.zeros((tok_rows, dec_wv.shape[1]), jnp.float32),
     )
     normed_part = (
-        lax.all_gather(sequence, "enc", axis=1, tiled=True).astype(jnp.float32)
+        press_columns_now(sequence, which_axis="enc").astype(jnp.float32)
         * row_scale[:, None]
         * dec_gain
     ).astype(jnp.bfloat16)

time: 496 us -> 544 us (1.097)
  waiting for transfers between devices: 259 us -> 303 us
  blocking collectives: 9.58 us -> 0 us
  starting transfers between devices: 17.1 us -> 26.4 us
  local copies, waits for them, and re-layouts: 46.6 us -> 52.6 us
    all_to_all x0 -> x1, waiting for transfers between devices: none -> 72 us  [press_columns_now(): k_now = lax.all_to_all(seen_now, which_axis, 0, 0)]
    all_gather x1 -> x0, waiting for transfers between devices: 30.6 us -> none  [body(): lax.all_gather(sequence, 'enc', axis=1, tiled=True).astype(jnp.float32)]
    all_to_all x1 -> x0, blocking collectives: 9.58 us -> none  [sent_to_all(): lax.all_to_all(jnp.broadcast_to(x[None], (size, *x.shape)), axis, 0, 0, t...]
    all_to_all x2 -> x3, waiting for transfers between devices: 42.2 us -> 47.2 us  [sent_to_all(): lax.all_to_all(jnp.broadcast_to(x[None], (size, *x.shape)), axis, 0, 0, t...]
    all_to_all x2 -> x3, starting transfers between devices: 9.78 us -> 14.2 us  [sent_to_all(): lax.all_to_all(jnp.broadcast_to(x[None], (size, *x.shape)), axis, 0, 0, t...]
  transfers between devices with their start and end apart: 6 -> 7, of which waited for: 6 -> 7; matrix products, arithmetic and copies ran while one was open for 3% -> 3% of each run, Pallas kernels for 0% -> 0%
where the time goes in v1:
time: 544 us; the launch traced here: 541 us
  waiting for transfers between devices  303 us (56%)
  matrix products  92.7 us (17%)
  local copies, waits for them, and re-layouts  52.6 us (10%)
  other arithmetic  45.4 us (8%)
  starting transfers between devices  26.4 us (5%)
  between operations  15.1 us (3%)
  loops' own time  6.57 us (1%)
    reduce_scatter x1, waiting for transfers between devices, body(): lax.psum_scatter(jnp.dot(picked, merge_down, preferred_element_type=jnp.f...  88.8 us
    all_to_all x1, waiting for transfers between devices, press_columns_now(): k_now = lax.all_to_all(seen_now, which_axis, 0, 0)  72 us
    all_to_all x1, waiting for transfers between devices, sent_and_summed(): lax.all_to_all(blocks, axis, split_axis=0, concat_axis=0, tiled=True)  59.5 us
    all_to_all x3, waiting for transfers between devices, sent_to_all(): lax.all_to_all(jnp.broadcast_to(x[None], (size, *x.shape)), axis, 0, 0, t...  47.2 us
    dot_general x12, matrix products, update_one_block(): jnp.einsum('gjts,sgd->gjtd', weights.astype(jnp.bfloat16), values_block,...  36.9 us
    all_gather x1, waiting for transfers between devices, in_one_piece(): result = lax.all_gather(both, axis, axis=dim, tiled=True)  35.1 us
    dot_general x12, matrix products, update_one_block(): jnp.einsum('gjtd,sgd->gjts', queries, keys_block, preferred_element_type=...  20.9 us
    add x12, other arithmetic, update_one_block(): totals = totals * factor + jnp.sum(weights, axis=3)  14.8 us
  transfers between devices with their start and end apart: 7, of which 7 were waited for; matrix products, arithmetic and copies ran while one was open for 3% of the time, Pallas kernels for 0%

profile of v1, /device:TPU:0, one launch (start us, length us, event | category | flops | bytes accessed | tf_op | source)
XLA Modules:
  0.0 541.4 jit_solution(17789890437050249063)
XLA Ops:
  6.6 2.0 convert_reduce_fusion
  11.3 2.0 copy.42
  13.3 1.9 slice_bitcast_fusion
  15.2 16.2 %while.28 = (s32[]{:T(128)}, bf16[3,1,256,80]{2,3,1,0:T(8,128)(2,1)}, s32[3]{0:T(128)S(1)}, s32[768]{0:T(1024)S(1)}, bf16[1,768,80]{2,1,0:T(8,128)(2,1)}, /*inde...) while((s32[]{:T(128)}, ...), condition=%wide.region_10.11_spmd, body=%wide.region_7.10_spmd.sunk | while | flops 64527876 | bytes 2797211 | solution.py:84
  32.5 3.5 fusion.81
  36.0 7.2 %all-to-all-start = ((f32[16,48,1280]{2,1,0:T(8,128)}), f32[16,48,1280]{2,1,0:T(8,128)}, u32[]{:S(2)}, u32[]{:S(2)}) async-start(f32[16,48,1280]{2,1,0:T(8,128)} %fusion.81), calls=%async_computation | async-start | bytes 7864320 | tf_op jit(solution)/shard_map/all_to_all | solution.py:21
  43.2 59.5 %all-to-all-done = f32[16,48,1280]{2,1,0:T(8,128)} async-done(((f32[16,48,1280]{2,1,0:T(8,128)}), f32[16,48,1280]{2,1,0:T(8,128)}, u32[]{:S(2)}, u32[]{:S(2)}) %all-to-all-start) | async-done | bytes 3932192 | tf_op jit(solution)/shard_map/all_to_all | solution.py:21
  102.7 2.3 reduce_sum.97
  107.9 4.5 all-to-all-start.1
  115.6 24.9 %all-to-all-done.1 = bf16[16,48,1280]{2,1,0:T(8,128)(2,1)} async-done(((bf16[16,48,1280]{2,1,0:T(8,128)(2,1)}), bf16[16,48,1280]{2,1,0:T(8,128)(2,1)}, u32[]{:S(2)}, u32[]{:S(2)}) %all-to-all-start.1) | async-done | bytes 1966112 | tf_op jit(solution)/shard_map/all_to_all | solution.py:33
  140.5 4.1 reshape_reshape.3
  144.6 3.6 fusion.68
  149.3 5.3 all-to-all-start.2
  154.7 17.3 %all-to-all-done.2 = bf16[8,192,320]{2,1,0:T(8,128)(2,1)S(1)} async-done(((bf16[8,192,320]{2,1,0:T(8,128)(2,1)}), bf16[8,192,320]{2,1,0:T(8,128)(2,1)S(1)}, u32[]{:S(2)}, u32[]{:S(2)}) %all-to-all-start.2) | async-done | bytes 983072 | tf_op jit(solution)/shard_map/all_to_all | solution.py:33
  171.9 11.0 %gather_fusion = bf16[3072,320]{1,0:T(8,128)(2,1)S(1)} fusion(bf16[1536,320]{1,0:T(8,128)(2,1)S(1)} %bitcast.157, s32[3072]{0:T(1024)S(1)} %broadcast_clamp_fusion), kind=kCustom, calls=%fused_computation | custom fusion | bytes 3944448 | tf_op jit(solution)/shard_map/jit(_take)/gather | solution.py:159
  182.9 7.6 %fusion.49 = f32[3072,1024]{1,0:T(8,128)} fusion(bf16[320,1024]{1,0:T(8,128)(2,1)} %param.28, bf16[3072,320]{1,0:T(8,128)(2,1)S(1)} %gather_fusion, pred[3072]{0:T(1024)(128)(4,1)} %compare_and_fusion.1, pred[3072]{0:T(1024)(128)(4,1)S(1)} %ge.77), kind=kOutput, calls=%fused_computation.63 | convolution fusion | flops 2015232000 | bytes 15210496 | tf_op jit(solution)/shard_map/dot_general | solution.py:162
  192.1 88.8 %reduce-scatter.2.cloned.1.call-done = f32[192,1024]{1,0:T(8,128)} async-done(((f32[3072,1024]{1,0:T(8,128)}), f32[192,1024]{1,0:T(8,128)}) %reduce-scatter.2.cloned.1.call-update) | async-done | bytes 786448 | tf_op jit(solution)/shard_map/reduce_scatter | solution.py:161
  282.1 2.1 gather_fusion.1
  285.4 4.4 all-to-all-start.4
  290.2 5.0 all-to-all-done.4
  295.1 3.2 stack.2
  298.3 4.9 all-to-all-start.3
  303.3 72.0 %all-to-all-done.3 = bf16[8,384,1024]{1,2,0:T(8,128)(2,1)} async-done(((bf16[8,384,1024]{1,2,0:T(8,128)(2,1)}), bf16[8,384,1024]{1,2,0:T(8,128)(2,1)}, u32[]{:S(2)}, u32[]{:S(2)}) %all-to-all-start.3) | async-done | bytes 6291488 | tf_op jit(solution)/shard_map/all_to_all | solution.py:109
  375.3 4.3 fusion.42
  388.8 8.8 %convolution_convert_fusion = bf16[384,512]{1,0:T(8,128)(2,1)S(1)} fusion(bf16[384,8192]{0,1:T(8,128)(2,1)} %copy-done.2, bf16[8192,512]{1,0:T(8,128)(2,1)} %param.33), kind=kOutput, calls=%fused_computation.73 | convolution fusion | flops 3221422080 | bytes 15073280 | tf_op jit(solution)/shard_map/dot_general | solution.py:183
  398.5 35.1 %all-gather.2.cloned.1.call-done = bf16[6144,256]{0,1:T(8,128)(2,1)} async-done(((bf16[384,256]{0,1:T(8,128)(2,1)}), bf16[6144,256]{0,1:T(8,128)(2,1)}) %all-gather.2.cloned.1.call-update) | async-done | bytes 3145744 | tf_op jit(solution)/shard_map/all_gather | solution.py:47
  433.6 98.2 %conditional.1 = (f32[1,4,384]{2,1,0:T(4,128)}, f32[1,4,384,128]{3,2,1,0:T(8,128)}) conditional(s32[]{:T(128)} %convert_element_type.81, () %tuple.31, (bf16[6144,256]{0,1:T(8,128)(2,1)}, s32[]{:T(128)}, s32[384]{0:T(512)S(1)}, s32[6144]{0:T(1024)}, s32[384]{0:T(512)S(1)}, /*index=5*/bf16[1,4,384,128]{3,2,1,0:T(8,128)(2,1)}) %tuple.85), branch_computations={%region_17.18_spmd, %region_18.23_spmd} | conditional | flops 412493696 | bytes 25149788 | solution.py:246
  433.6 3.2 copy.47
  436.8 1.9 fusion.89
  438.7 93.2 %while.27 = (s32[]{:T(128)}, f32[1,4,384]{2,1,0:T(4,128)S(1)}, f32[1,4,384]{2,1,0:T(4,128)}, f32[1,4,384,128]{3,2,1,0:T(8,128)}, s32[384]{0:T(512)S(1)}, /*index...) while((s32[]{:T(128)}, f32[1,4,384]{2,1,0:T(4,128)S(1)}, ...), condition=%wide.region_22.22_spmd.clone, body=%wide.region_19.21_spmd.clone.sunk | while | flops 412493312 | bytes 12563663 | solution.py:241
  441.4 2.8 fusion.121
  448.3 3.1 fusion.121
  456.1 3.1 fusion.121
  462.2 1.7 fusion.118
  464.0 3.1 fusion.121
  470.1 1.7 fusion.118
  471.8 3.1 fusion.121
  477.9 1.7 fusion.118
  479.7 3.1 fusion.121
  485.7 1.7 fusion.118
  487.5 3.1 fusion.121
  495.4 3.1 fusion.121
  503.2 3.1 fusion.121
  511.1 3.1 fusion.121
  517.1 1.7 fusion.118
  518.9 3.1 fusion.121
  525.0 1.7 fusion.118
  526.8 3.1 fusion.121
  (200 shorter events, 82.0 us)
Async XLA Ops:
  6.5 138.1 %copy-start = (bf16[5120,320]{0,1:T(8,128)(2,1)S(1)}, bf16[5120,320]{0,1:T(8,128)(2,1)}, u32[]{:S(2)}) copy-start(bf16[5120,320]{0,1:T(8,128)(2,1)} %param.27) | copy-start | bytes 9830404
  6.5 3.0 copy-start.12
  6.5 2.3 copy-start.3
  6.5 3.0 copy-start.11
  9.5 5.7 %copy-start.8 = (s32[768]{0:T(1024)S(1)}, s32[768]{0:T(1024)}, u32[]{:S(2)}) copy-start(s32[768]{0:T(1024)} %param.22) | copy-start | bytes 9220
  36.0 66.7 %all-to-all-start = ((f32[16,48,1280]{2,1,0:T(8,128)}), f32[16,48,1280]{2,1,0:T(8,128)}, u32[]{:S(2)}, u32[]{:S(2)}) async-start(f32[16,48,1280]{2,1,0:T(8,128)} %fusion.81), calls=%async_computation | async-start | bytes 7864320 | tf_op jit(solution)/shard_map/all_to_all | solution.py:21
  43.2 63.2 %copy-start.7 = (f32[1280]{0:T(1024)S(1)}, f32[1280]{0:T(1024)}, u32[]{:S(2)}) copy-start(f32[1280]{0:T(1024)} %param.26) | copy-start | bytes 15364
  106.3 6.0 %copy-start.5 = (s32[6144]{0:T(1024)S(1)}, s32[6144]{0:T(1024)}, u32[]{:S(2)}) copy-start(s32[6144]{0:T(1024)} %param.30) | copy-start | bytes 73732
  107.9 32.7 %all-to-all-start.1 = ((bf16[16,48,1280]{2,1,0:T(8,128)(2,1)}), bf16[16,48,1280]{2,1,0:T(8,128)(2,1)}, u32[]{:S(2)}, u32[]{:S(2)}) async-start(bf16[16,48,1280]{2,1,0:T(8,128)(2,1)} %broadcast_in_dim.157), calls=%async_computation.1 | async-start | bytes 3932160 | tf_op jit(solution)/shard_map/all_to_all | solution.py:33
  149.3 22.6 %all-to-all-start.2 = ((bf16[8,192,320]{2,1,0:T(8,128)(2,1)}), bf16[8,192,320]{2,1,0:T(8,128)(2,1)S(1)}, u32[]{:S(2)}, u32[]{:S(2)}) async-start(bf16[8,192,320]{2,1,0:T(8,128)(2,1)} %broadcast_in_dim.158), calls=%async_computation.2 | async-start | bytes 2359296 | tf_op jit(solution)/shard_map/all_to_all | solution.py:33
  154.6 126.3 %reduce-scatter.2.cloned.1.call-start = ((), (), s32[]{:S(2)}) async-start(), calls=%async_computation.6 | async-start | bytes 13369344 | tf_op jit(solution)/shard_map/reduce_scatter | solution.py:161
  282.1 2.1 copy-start.4
  285.4 9.8 %all-to-all-start.4 = ((f32[8,1,384]{2,1,0:T(1,128)}), f32[8,1,384]{2,1,0:T(1,128)S(1)}, u32[]{:S(2)}, u32[]{:S(2)}) async-start(f32[8,1,384]{2,1,0:T(1,128)} %broadcast_in_dim.162), calls=%async_computation.5 | async-start | bytes 24576 | tf_op jit(solution)/shard_map/all_to_all | solution.py:33
  298.3 77.0 %copy-start.6 = (f32[8192]{0:T(1024)S(1)}, f32[8192]{0:T(1024)}, u32[]{:S(2)}) copy-start(f32[8192]{0:T(1024)} %param.32) | copy-start | bytes 98308
  298.3 77.0 %all-to-all-start.3 = ((bf16[8,384,1024]{1,2,0:T(8,128)(2,1)}), bf16[8,384,1024]{1,2,0:T(8,128)(2,1)}, u32[]{:S(2)}, u32[]{:S(2)}) async-start(bf16[8,384,1024]{1,2,0:T(8,128)(2,1)} %stack.2), calls=%async_computation.4 | async-start | bytes 12582912 | tf_op jit(solution)/shard_map/all_to_all | solution.py:109
  303.2 130.4 %all-gather.2.cloned.1.call-start = ((), (), s32[]{:S(2)}) async-start(), calls=%async_computation.7 | async-start | bytes 3342336 | tf_op jit(solution)/shard_map/all_gather | solution.py:47
  303.3 76.3 %copy-start.9 = (bf16[8192,128]{1,0:T(8,128)(2,1)S(1)}, bf16[8192,128]{1,0:T(8,128)(2,1)}, u32[]{:S(2)}) copy-start(bf16[8192,128]{1,0:T(8,128)(2,1)} %param.35) | copy-start | bytes 6291460
  379.6 2.9 copy-start.2
  379.6 3.2 copy-start.10
  531.8 2.7 copy-start.1
Sparse Core Ops, SparseCore 0:
  190.7 90.1 reduce-scatter.1
  384.9 48.6 all-gather.1
